TPU v7x, 32 devices: a whole 2x2x4 slice. The times are simulated.
32 devices in a mesh: dp: 8 (over z, x), expert: 4 (over y, core).
Axes of the slice: x: 2, y: 2, z: 4, core: 2. Of those that a mesh axis runs over, the one named last changes fastest.
Arguments:
- tokens: bfloat16 [1024, 4096], P('expert', 'dp'), may hold values from -6 to 6
- cotangent: bfloat16 [1024, 4096], P('expert', 'dp'), may hold values from -6 to 6
- expert_ids: int32 [1024, 2], P('expert'), may hold values from 0 to 3, all different within a row; in each aligned block of 256 rows (0 to 255, 256 to 511, ...) at most 129 rows name the same one
- combine: float32 [1024, 2], P('expert'), may hold values from 0.1 to 1
- w_gate: bfloat16 [4, 4096, 14336], P('expert', None, 'dp'), may hold values from -0.09375 to 0.09375
- w_up: bfloat16 [4, 4096, 14336], P('expert', None, 'dp'), may hold values from -0.09375 to 0.09375
- w_down: bfloat16 [4, 14336, 4096], P('expert', 'dp'), may hold values from -0.046875 to 0.046875
- scale_vector: float32 [4, 14336], P('expert', 'dp'), may hold values from 0.25 to 1.75
Outputs:
- token_grads: bfloat16 [1024, 4096], P('expert', 'dp')
- scale_grads: float32 [4, 14336], P('expert', 'dp')
Inputs may be any that keep to these rules, and one draw needn't show every extreme that they name: `expert_ids`: each row names 2 different experts. Among the 256 rows of one aligned block no expert is named more than 129 times, and some block names some expert exactly 129 times.
All inputs are finite; a program needn't handle non-finite values.
Results may differ from a plain program's by a relative error of at most 0.0065.
Values may be sent and summed in bfloat16 or wider, within the bound.
A program may use at most 128 MiB of HBM per device.

v0:
```python
import jax
import jax.numpy as jnp
from jax import lax
from jax.sharding import PartitionSpec as P


def route_tables(expert_ids, combine, experts, capacity):
    blocks = expert_ids.shape[0]
    per_block = expert_ids.shape[1]
    onehot = (expert_ids[:, :, :, None] == jnp.arange(experts, dtype=jnp.int32)).astype(jnp.int32)
    flat_hits = onehot.reshape(blocks, per_block * 2, experts)
    earlier = jnp.cumsum(flat_hits, axis=1) - flat_hits
    slot_ids = jnp.sum(earlier * flat_hits, axis=2).reshape(blocks, per_block, 2)
    positions = (slot_ids[:, :, :, None] == jnp.arange(capacity, dtype=jnp.int32)).astype(
        jnp.float32
    )
    matches = onehot.astype(jnp.float32)[:, :, :, :, None] * positions[:, :, :, None, :]
    dispatch = jnp.transpose(jnp.sum(matches, axis=2), (0, 2, 3, 1))
    slot_weight = jnp.sum(matches * combine[:, :, :, None, None], axis=(1, 2))
    return (dispatch, slot_weight, slot_ids)


def combine_slots(slot_table, flat_index):
    tok_count = flat_index.shape[0]
    picked = jnp.take(slot_table, flat_index.reshape(-1), axis=0).reshape(
        tok_count, 2, slot_table.shape[1]
    )
    return picked[:, 0] + picked[:, 1]


def local(tokens, cotangent, expert_ids, combine, w_gate, w_up, w_down, scale_vector):
    experts = lax.axis_size("expert")
    tok_count = tokens.shape[0]
    capacity = 2 * tok_count // experts + 1
    dispatch, slot_weight, slot_ids = route_tables(
        expert_ids[None], combine[None], experts, capacity
    )
    dispatch_half = dispatch[0].astype(jnp.bfloat16)
    slot_weight = slot_weight[0]
    flat_index = expert_ids * capacity + slot_ids[0]
    sent_rows = jnp.einsum(
        "ect,td->ecd", dispatch_half, tokens, preferred_element_type=jnp.float32
    ).astype(jnp.bfloat16)
    cot_rows = jnp.einsum(
        "ect,td->ecd", dispatch_half, cotangent, preferred_element_type=jnp.float32
    )
    sent_grads = (slot_weight[:, :, None] * cot_rows).astype(jnp.bfloat16)
    got_rows, got_grads = (
        lax.all_to_all(sent_rows, "expert", split_axis=0, concat_axis=0, tiled=True),
        lax.all_to_all(sent_grads, "expert", split_axis=0, concat_axis=0, tiled=True),
    )
    row_count = experts * capacity
    gate_w = w_gate[0]
    up_w = w_up[0]
    down_w = w_down[0]
    rows_piece = lax.all_gather(got_rows, "dp", axis=2, tiled=True)
    grads_piece = lax.all_gather(got_grads, "dp", axis=2, tiled=True)
    piece_width = rows_piece.shape[2]
    rows_flat = rows_piece.reshape(row_count, piece_width)
    grads_flat = grads_piece.reshape(row_count, piece_width)
    gate_act = jnp.dot(rows_flat, gate_w, preferred_element_type=jnp.float32)
    up_act = jnp.dot(rows_flat, up_w, preferred_element_type=jnp.float32)
    hidden_grad = lax.dot_general(
        grads_flat, down_w, (((1,), (1,)), ((), ())), preferred_element_type=jnp.float32
    )
    sigmoid_gate = jax.nn.sigmoid(gate_act)
    silu_gate = gate_act * sigmoid_gate
    scale_grad = jnp.sum(hidden_grad * silu_gate * up_act, axis=0)
    scaled_grad = hidden_grad * scale_vector[0]
    up_grad = (scaled_grad * silu_gate).astype(jnp.bfloat16)
    gate_grad = (
        scaled_grad * up_act * sigmoid_gate * (1.0 + gate_act * (1.0 - sigmoid_gate))
    ).astype(jnp.bfloat16)
    partial_value = lax.dot_general(
        gate_grad, gate_w, (((1,), (1,)), ((), ())), preferred_element_type=jnp.float32
    ) + lax.dot_general(up_grad, up_w, (((1,), (1,)), ((), ())), preferred_element_type=jnp.float32)
    summed = lax.psum_scatter(partial_value, "dp", scatter_dimension=1, tiled=True)
    slot_part = summed.reshape(experts, capacity, summed.shape[1])
    returned = lax.all_to_all(slot_part, "expert", split_axis=0, concat_axis=0, tiled=True)
    token_grads = combine_slots(returned.reshape(row_count, returned.shape[2]), flat_index)
    return (token_grads.astype(jnp.bfloat16), scale_grad[None, :])


def solution(mesh):
    placed = (
        P("expert", "dp"),
        P("expert", "dp"),
        P("expert", None),
        P("expert", None),
        P("expert", None, "dp"),
        P("expert", None, "dp"),
        P("expert", "dp", None),
        P("expert", "dp"),
    )
    return jax.shard_map(
        local,
        mesh=mesh,
        in_specs=placed,
        out_specs=(P("expert", "dp"), P("expert", "dp")),
        check_vma=False,
    )
```

profile of v0, /device:TPU:0, one launch (start us, length us, event | category | flops | bytes accessed | tf_op | source)
XLA Modules:
  0.0 428.5 jit_solution(7830749890703558208)
XLA Ops:
  7.2 0.9 copy.30
  8.3 1.2 reduce-window.6
  9.7 0.7 convert_convert_fusion
  11.0 1.4 fusion.18
  12.4 0.3 fusion.17
  12.8 13.3 %all_to_all.15 = bf16[4,129,512]{2,1,0:T(8,128)(2,1)} all-to-all(bf16[4,129,512]{2,1,0:T(8,128)(2,1)S(1)} %fusion.17), channel_id=1, replica_groups=mesh['dp'=8,'expert'=4] {'expert'}, dimensions={0} | all-to-all | bytes 1056768 | tf_op jit(solution)/shard_map/all_to_all | solution.py:50
  26.5 12.3 %all_to_all.16 = bf16[4,129,512]{2,1,0:T(8,128)(2,1)} all-to-all(bf16[4,129,512]{2,1,0:T(8,128)(2,1)S(1)} %convolution_convert_fusion), channel_id=1, replica_groups=mesh['dp'=8,'expert'=4] {'expert'}, dimensions={0} | all-to-all | bytes 1056768 | tf_op jit(solution)/shard_map/all_to_all | solution.py:49
  38.9 65.7 %all-gather.3.cloned.1.call-done = bf16[4,129,4096]{2,1,0:T(8,128)(2,1)} async-done(((bf16[4,129,512]{2,1,0:T(8,128)(2,1)}), bf16[4,129,4096]{2,1,0:T(8,128)(2,1)}) %all-gather.3.cloned.1.call-update) | async-done | bytes 4227088 | tf_op jit(solution)/shard_map/all_gather | solution.py:57
  104.6 5.3 %reshape.201 = bf16[516,4096]{1,0:T(8,128)(2,1)} reshape(bf16[4,129,4096]{2,1,0:T(8,128)(2,1)} %all-gather.3.cloned.1.call-done) | data formatting | bytes 8454144 | tf_op jit(solution)/shard_map/reshape | solution.py:60
  109.9 15.3 %fusion.8 = f32[516,1792]{1,0:T(8,128)} fusion(bf16[516,4096]{1,0:T(8,128)(2,1)} %reshape.201, bf16[1,1792,4096]{2,1,0:T(8,128)(2,1)} %param.14), kind=kOutput, calls=%fused_computation.9 | convolution fusion | flops 7574913024 | bytes 22605824 | tf_op jit(solution)/shard_map/dot_general | solution.py:63
  125.2 57.2 %all-gather.5.cloned.1.call-done = bf16[4,129,4096]{2,1,0:T(8,128)(2,1)} async-done(((bf16[4,129,512]{2,1,0:T(8,128)(2,1)}), bf16[4,129,4096]{2,1,0:T(8,128)(2,1)}) %all-gather.5.cloned.1.call-update) | async-done | bytes 4227088 | tf_op jit(solution)/shard_map/all_gather | solution.py:56
  182.4 5.4 %reshape.202 = bf16[516,4096]{1,0:T(8,128)(2,1)} reshape(bf16[4,129,4096]{2,1,0:T(8,128)(2,1)} %all-gather.5.cloned.1.call-done) | data formatting | bytes 8454144 | tf_op jit(solution)/shard_map/reshape | solution.py:59
  187.9 12.0 %fusion.2 = f32[516,1792]{1,0:T(8,128)S(1)} fusion(bf16[516,4096]{1,0:T(8,128)(2,1)} %reshape.202, bf16[1,4096,1792]{2,1,0:T(8,128)(2,1)} %param.12), kind=kOutput, calls=%fused_computation.3 | convolution fusion | flops 7574913024 | bytes 22605824 | tf_op jit(solution)/shard_map/dot_general | solution.py:61
  199.9 15.3 %multiply_reduce_fusion = (f32[1792]{0:T(1024)S(1)}, f32[516,1792]{1,0:T(8,128)}) fusion(f32[516,1792]{1,0:T(8,128)S(1)} %copy-done.6, f32[516,1792]{1,0:T(8,128)S(1)} %fusion.2, bf16[516,4096]{1,0:T(8,128)(2,1)S(1)} %copy-done.2, bf16[1,4096,1792]{2,1,0:T(8,128)(2,1)} %param.13), kind=kOutput, calls=%fused_computation.12 | convolution fusion | flops 7581383680 | bytes 30010368 | tf_op jit(solution)/shard_map/dot_general | solution.py:62
  215.2 17.5 %fusion = f32[516,4096]{1,0:T(8,128)} fusion(bf16[1,4096,1792]{2,1,0:T(8,128)(2,1)} %param.12, f32[516,1792]{1,0:T(8,128)} %copy-done.7, f32[516,1792]{1,0:T(8,128)} %get-tuple-element.7, f32[516,1792]{1,0:T(8,128)} %fusion.8, f32[1792]{0:T(1024)S(1)} %reduce.4), kind=kOutput, calls=%fused_computation.1 | convolution fusion | flops 7585084416 | bytes 34237440 | tf_op jit(solution)/shard_map/dot_general | solution.py:74
  232.7 16.6 %fusion.10 = f32[516,4096]{1,0:T(8,128)} fusion(f32[516,4096]{1,0:T(8,128)} %fusion, bf16[1,4096,1792]{2,1,0:T(8,128)(2,1)} %param.13, f32[516,1792]{1,0:T(8,128)} %fusion.8, f32[1792]{0:T(1024)S(1)} %reduce.4, f32[516,1792]{1,0:T(8,128)} %copy-done.7), kind=kOutput, calls=%fused_computation.11 | convolution fusion | flops 7583499264 | bytes 38992896 | tf_op jit(solution)/shard_map/dot_general | solution.py:76
  249.4 148.1 %reduce-scatter.2.cloned.1.call-done = f32[516,512]{1,0:T(8,128)} async-done(((f32[516,4096]{1,0:T(8,128)}), f32[516,512]{1,0:T(8,128)}) %reduce-scatter.2.cloned.1.call-update) | async-done | bytes 1056784 | tf_op jit(solution)/shard_map/reduce_scatter | solution.py:77
  397.5 2.4 reshape.203
  399.9 3.5 all-to-all-start.2
  403.7 0.6 broadcast_in_dim.19
  404.3 14.2 %all-to-all-done.2 = f32[4,129,512]{2,1,0:T(8,128)S(1)} async-done(((f32[4,129,512]{2,1,0:T(8,128)}), f32[4,129,512]{2,1,0:T(8,128)S(1)}, u32[]{:S(2)}, u32[]{:S(2)}) %all-to-all-start.2) | async-done | bytes 1056800 | tf_op jit(solution)/shard_map/all_to_all | solution.py:79
  418.7 1.6 gather_fusion
  420.3 0.6 gather.7
  421.2 0.8 fusion.22
  (45 shorter events, 2.3 us)
Async XLA Ops:
  7.2 5.3 %copy-start = (bf16[256,512]{1,0:T(8,128)(2,1)S(1)}, bf16[256,512]{1,0:T(8,128)(2,1)}, u32[]{:S(2)}) copy-start(bf16[256,512]{1,0:T(8,128)(2,1)} %param.9) | copy-start | bytes 786436
  7.2 19.0 %copy-start.3 = (bf16[256,512]{1,0:T(8,128)(2,1)S(1)}, bf16[256,512]{1,0:T(8,128)(2,1)}, u32[]{:S(2)}) copy-start(bf16[256,512]{1,0:T(8,128)(2,1)} %param.8) | copy-start | bytes 786436
  7.2 31.6 %copy-start.5 = (f32[1,1792]{1,0:T(1,128)S(1)}, f32[1,1792]{1,0:T(1,128)}, u32[]{:S(2)}) copy-start(f32[1,1792]{1,0:T(1,128)} %param.15) | copy-start | bytes 21508
  7.2 97.4 %all-gather.3.cloned.1.call-start = ((), (), s32[]{:S(2)}) async-start(), calls=%async_computation.4 | async-start | bytes 5013504 | tf_op jit(solution)/shard_map/all_gather | solution.py:57
  26.1 156.3 %all-gather.5.cloned.1.call-start = ((), (), s32[]{:S(2)}) async-start(), calls=%async_computation.5 | async-start | bytes 5013504 | tf_op jit(solution)/shard_map/all_gather | solution.py:56
  38.8 358.7 %reduce-scatter.2.cloned.1.call-start = ((), (), s32[]{:S(2)}) async-start(), calls=%async_computation.6 | async-start | bytes 9584640 | tf_op jit(solution)/shard_map/reduce_scatter | solution.py:77
  187.8 12.0 %copy-start.2 = (bf16[516,4096]{1,0:T(8,128)(2,1)S(1)}, bf16[516,4096]{1,0:T(8,128)(2,1)}, u32[]{:S(2)}) copy-start(bf16[516,4096]{1,0:T(8,128)(2,1)} %reshape.202) | copy-start | bytes 12681220
  187.8 12.0 %copy-start.6 = (f32[516,1792]{1,0:T(8,128)S(1)}, f32[516,1792]{1,0:T(8,128)}, u32[]{:S(2)}) copy-start(f32[516,1792]{1,0:T(8,128)} %fusion.8) | copy-start | bytes 11096068
  199.9 15.3 %copy-start.7 = (f32[516,1792]{1,0:T(8,128)}, f32[516,1792]{1,0:T(8,128)S(1)}, u32[]{:S(2)}) copy-start(f32[516,1792]{1,0:T(8,128)S(1)} %fusion.2) | copy-start | bytes 11096068
  249.4 154.0 %copy-start.4 = (s32[256,2]{0,1:T(2,128)S(1)}, s32[256,2]{0,1:T(2,128)}, u32[]{:S(2)}) copy-start(s32[256,2]{0,1:T(2,128)} %param.10) | copy-start | bytes 6148
  399.9 18.6 %all-to-all-start.2 = ((f32[4,129,512]{2,1,0:T(8,128)}), f32[4,129,512]{2,1,0:T(8,128)S(1)}, u32[]{:S(2)}, u32[]{:S(2)}) async-start(f32[4,129,512]{2,1,0:T(8,128)} %reshape.203), calls=%async_computation.3 | async-start | bytes 2228224 | tf_op jit(solution)/shard_map/all_to_all | solution.py:79
  418.7 3.3 copy-start.1
Sparse Core Ops, SparseCore 0:
  26.2 78.2 all-gather.2
  106.6 75.7 all-gather.4
  249.5 147.9 reduce-scatter.1
where the time goes:
time: 429 us
  waiting for transfers between devices  285 us (66%)
  matrix products  77.4 us (18%)
  blocking collectives  25.6 us (6%)
  local copies, waits for them, and re-layouts  18.1 us (4%)
  between operations  14 us (3%)
  other arithmetic  4.6 us (1%)
    reduce_scatter x1, waiting for transfers between devices, local(): lax.psum_scatter(partial_value, 'dp', scatter_dimension=1, tiled=True)  148 us
    all_gather x1, waiting for transfers between devices, local(): grads_piece = lax.all_gather(got_grads, 'dp', axis=2, tiled=True)  65.7 us
    all_gather x1, waiting for transfers between devices, local(): rows_piece = lax.all_gather(got_rows, 'dp', axis=2, tiled=True)  57.2 us
    dot_general x1, matrix products, local(): lax.dot_general(gate_grad, gate_w, (((1,), (1,)), ((), ())), preferred_el...  17.5 us
    dot_general x1, matrix products, local(): lax.dot_general(up_grad, up_w, (((1,), (1,)), ((), ())), preferred_elemen...  16.6 us
    dot_general x1, matrix products, local(): lax.dot_general(grads_flat, down_w, (((1,), (1,)), ((), ())), preferred_e...  15.3 us
    dot_general x1, matrix products, local(): up_act = jnp.dot(rows_flat, up_w, preferred_element_type=jnp.float32)  15.3 us
    all_to_all x1, waiting for transfers between devices, local(): lax.all_to_all(slot_part, 'expert', split_axis=0, concat_axis=0, tiled=True)  14.2 us
  transfers between devices with their start and end apart: 4, of which 4 were waited for; matrix products, arithmetic and copies ran while one was open for 5% of the time, Pallas kernels for 0%

commit v1 on v0

--- a/solution.py
+++ b/solution.py
@@ -1,6 +1,10 @@
+import functools
+
 import jax
 import jax.numpy as jnp
 from jax import lax
+from jax.experimental import pallas as pl
+from jax.experimental.pallas import tpu as pltpu
 from jax.sharding import PartitionSpec as P
 
 
@@ -25,10 +29,314 @@
     picked = jnp.take(slot_table, flat_index.reshape(-1), axis=0).reshape(
         tok_count, 2, slot_table.shape[1]
     )
-    return picked[:, 0] + picked[:, 1]
-
-
-def local(tokens, cotangent, expert_ids, combine, w_gate, w_up, w_down, scale_vector):
+    return picked[:, 0].astype(jnp.float32) + picked[:, 1].astype(jnp.float32)
+
+
+MESH = pl.DeviceIdType.MESH
+ROW_TILE = 16
+SHORT_RING = 8
+VMEM_LIMIT = 60 * 1024 * 1024
+
+
+def ring_order(mesh):
+    count = mesh.shape["dp"]
+    devices = mesh.devices.reshape(count, -1)[:, 0]
+    places = {}
+    for index, device in enumerate(devices):
+        coords = getattr(device, "coords", None)
+        if coords is None:
+            return tuple(range(count))
+        places[(coords[2], coords[0])] = index
+    zs = sorted({z for z, _ in places})
+    xs = sorted({x for _, x in places})
+    if len(places) != count or len(zs) * len(xs) != count or len(zs) % 2 or len(xs) < 2:
+        return tuple(range(count))
+    order = [places[(z, xs[0])] for z in zs]
+    for turn, z in enumerate(reversed(zs)):
+        order += [places[(z, x)] for x in (xs[1:] if turn % 2 == 0 else xs[:0:-1])]
+    return tuple(order)
+
+
+def lookup(table, key):
+    found = jnp.int32(table[0])
+    for index in range(1, len(table)):
+        found = jnp.where(key == index, jnp.int32(table[index]), found)
+    return found
+
+
+def ring_place(ring):
+    n = len(ring)
+    position_of = [0] * n
+    for position, index in enumerate(ring):
+        position_of[index] = position
+    position = lookup(position_of, lax.axis_index("dp"))
+    right = lookup(ring, lax.rem(position + 1, n))
+    left = lookup(ring, lax.rem(position + n - 1, n))
+    return position, right, left
+
+
+def greet(right, left):
+    barrier = pltpu.get_barrier_semaphore()
+    for neighbour in (left, right):
+        pl.semaphore_signal(barrier, inc=1, device_id={"dp": neighbour}, device_id_type=MESH)
+    pl.semaphore_wait(barrier, 2)
+
+
+def gather_kernel(
+    ring, tile, x_ref, gate_w, up_w, gate_ref, up_ref, grads_ref, rows_ref, w_buf, w_sem, own_sem,
+    send_sem, recv_sem,
+):
+    n = len(ring)
+    width = x_ref.shape[1] // 2
+    rows = x_ref.shape[0]
+    cut = rows // 2 // ROW_TILE * ROW_TILE
+    tiles = gate_w.shape[1] // tile
+    position, right, left = ring_place(ring)
+    me = lax.axis_index("dp")
+    halves = (pl.ds(0, cut), pl.ds(cut, rows - cut))
+
+    def tile_columns(t):
+        return pl.ds(0, tile) if tiles == 1 else pl.ds(pl.multiple_of(t * tile, tile), tile)
+
+    def load(t, slot):
+        columns = tile_columns(t)
+        return (
+            pltpu.make_async_copy(gate_w.at[:, columns], w_buf.at[slot, 0], w_sem.at[slot, 0]),
+            pltpu.make_async_copy(up_w.at[:, columns], w_buf.at[slot, 1], w_sem.at[slot, 1]),
+        )
+
+    for copy in load(0, 0):
+        copy.start()
+
+    def columns_of(index):
+        return pl.ds(pl.multiple_of(index * width, width), width)
+
+    for which, full in enumerate((rows_ref, grads_ref)):
+        own = pltpu.make_async_copy(
+            x_ref.at[:, pl.ds(which * width, width)], full.at[:, columns_of(me)], own_sem.at[which]
+        )
+        own.start()
+        own.wait()
+    greet(right, left)
+
+    def hop(which, step, way):
+        full = (rows_ref, grads_ref)[which]
+        shift = n - step if way == 0 else step
+        origin = lookup(ring, lax.rem(position + shift, n))
+        spot = full.at[halves[way], columns_of(origin)]
+        return pltpu.make_async_remote_copy(
+            src_ref=spot,
+            dst_ref=spot,
+            send_sem=send_sem.at[which, way, step],
+            recv_sem=recv_sem.at[which, way, step],
+            device_id={"dp": right if way == 0 else left},
+            device_id_type=MESH,
+        )
+
+    def advance(which, step):
+        for way in range(2):
+
+            @pl.when(step > 0)
+            def _():
+                hop(which, step - 1, way).wait_recv()
+
+            hop(which, step, way).start()
+
+    def rows_step(step, carry):
+        advance(0, step)
+        return carry
+
+    lax.fori_loop(0, n - 1, rows_step, 0)
+    for way in range(2):
+        hop(1, 0, way).start()
+    for way in range(2):
+        hop(0, n - 2, way).wait_recv()
+
+    def grads_step(step, carry):
+        @pl.when(step > 0)
+        def _():
+            advance(1, step)
+
+        @pl.when(step < tiles)
+        def _():
+            slot = lax.rem(step, 2)
+
+            @pl.when(step + 1 < tiles)
+            def _():
+                for copy in load(step + 1, lax.rem(step + 1, 2)):
+                    copy.start()
+
+            columns = tile_columns(step)
+            for copy in load(step, slot):
+                copy.wait()
+            gate_ref[:, columns] = jnp.dot(
+                rows_ref[...], w_buf[slot, 0], preferred_element_type=jnp.float32
+            )
+            up_ref[:, columns] = jnp.dot(
+                rows_ref[...], w_buf[slot, 1], preferred_element_type=jnp.float32
+            )
+
+        return carry
+
+    lax.fori_loop(0, n - 1, grads_step, 0)
+    for way in range(2):
+        hop(1, n - 2, way).wait_recv()
+
+    def finish(step, carry):
+        for which in range(2):
+            for way in range(2):
+                hop(which, step, way).wait_send()
+        return carry
+
+    lax.fori_loop(0, n - 1, finish, 0)
+
+
+def gather_acts(ring, x, gate_w, up_w):
+    n = len(ring)
+    rows, width = x.shape[0], x.shape[1] // 2
+    hidden = gate_w.shape[1]
+    tile = 256 if hidden % 256 == 0 and hidden // 256 <= n - 1 else hidden
+    full = n * width
+    vmem = pl.BlockSpec(memory_space=pltpu.VMEM)
+    anywhere = pl.BlockSpec(memory_space=pl.ANY)
+    return pl.pallas_call(
+        functools.partial(gather_kernel, ring, tile),
+        out_shape=(
+            jax.ShapeDtypeStruct((rows, hidden), jnp.float32),
+            jax.ShapeDtypeStruct((rows, hidden), jnp.float32),
+            jax.ShapeDtypeStruct((rows, full), jnp.bfloat16),
+        ),
+        in_specs=[anywhere, anywhere, anywhere],
+        out_specs=(vmem, vmem, vmem),
+        scratch_shapes=[
+            pltpu.VMEM((rows, full), jnp.bfloat16),
+            pltpu.VMEM((2, 2, full, tile), jnp.bfloat16),
+            pltpu.SemaphoreType.DMA((2, 2)),
+            pltpu.SemaphoreType.DMA((2,)),
+            pltpu.SemaphoreType.DMA((2, 2, n - 1)),
+            pltpu.SemaphoreType.DMA((2, 2, n - 1)),
+        ],
+        compiler_params=pltpu.CompilerParams(
+            collective_id=0, has_side_effects=True, vmem_limit_bytes=VMEM_LIMIT
+        ),
+    )(x, gate_w, up_w)
+
+
+def scatter_kernel(
+    ring, gate_grad, up_grad, gate_w, up_w, out_ref, buf, w_buf, w_sem, send_sem, recv_sem
+):
+    n = len(ring)
+    half = buf.shape[3]
+    position, right, left = ring_place(ring)
+
+    def load(step, slot):
+        copies = []
+        for way in range(2):
+            shift = 2 * n - 1 - step if way == 0 else 1 + step
+            owner = lookup(ring, lax.rem(position + shift, n))
+            lines = pl.ds(pl.multiple_of(owner * (2 * half) + way * half, half), half)
+            for kind, weight in enumerate((gate_w, up_w)):
+                copies.append(
+                    pltpu.make_async_copy(
+                        weight.at[lines, :], w_buf.at[slot, way, kind], w_sem.at[slot, way, kind]
+                    )
+                )
+        return copies
+
+    for copy in load(0, 0):
+        copy.start()
+    greet(right, left)
+
+    def hop(step, way):
+        return pltpu.make_async_remote_copy(
+            src_ref=buf.at[way, step],
+            dst_ref=buf.at[way, step + 1],
+            send_sem=send_sem.at[way, step],
+            recv_sem=recv_sem.at[way, step],
+            device_id={"dp": right if way == 0 else left},
+            device_id_type=MESH,
+        )
+
+    def product(slot, way):
+        across = (((1,), (1,)), ((), ()))
+        return lax.dot_general(
+            gate_grad[...], w_buf[slot, way, 0], across, preferred_element_type=jnp.float32
+        ) + lax.dot_general(
+            up_grad[...], w_buf[slot, way, 1], across, preferred_element_type=jnp.float32
+        )
+
+    def one_step(step, carry):
+        slot = lax.rem(step, 2)
+
+        @pl.when(step + 1 < n)
+        def _():
+            for copy in load(step + 1, lax.rem(step + 1, 2)):
+                copy.start()
+
+        for copy in load(step, slot):
+            copy.wait()
+        for way in range(2):
+            part = product(slot, way)
+
+            @pl.when(step == 0)
+            def _():
+                buf[way, 0] = part.astype(buf.dtype)
+
+            @pl.when(step > 0)
+            def _():
+                hop(step - 1, way).wait_recv()
+                total = buf[way, step].astype(jnp.float32) + part
+
+                @pl.when(step < n - 1)
+                def _():
+                    buf[way, step] = total.astype(buf.dtype)
+
+                @pl.when(step == n - 1)
+                def _():
+                    out_ref[way] = total.astype(out_ref.dtype)
+
+            @pl.when(step < n - 1)
+            def _():
+                hop(step, way).start()
+
+        return carry
+
+    lax.fori_loop(0, n, one_step, 0)
+
+    def finish(step, carry):
+        for way in range(2):
+            hop(step, way).wait_send()
+        return carry
+
+    lax.fori_loop(0, n - 1, finish, 0)
+
+
+def scatter_rows(ring, gate_grad, up_grad, gate_w, up_w):
+    n = len(ring)
+    rows, hidden = gate_grad.shape
+    half = gate_w.shape[0] // n // 2
+    wire = jnp.bfloat16 if n <= SHORT_RING else jnp.float32
+    vmem = pl.BlockSpec(memory_space=pltpu.VMEM)
+    anywhere = pl.BlockSpec(memory_space=pl.ANY)
+    return pl.pallas_call(
+        functools.partial(scatter_kernel, ring),
+        out_shape=jax.ShapeDtypeStruct((2, rows, half), wire),
+        in_specs=[vmem, vmem, anywhere, anywhere],
+        out_specs=vmem,
+        scratch_shapes=[
+            pltpu.VMEM((2, n, rows, half), wire),
+            pltpu.VMEM((2, 2, 2, half, hidden), jnp.bfloat16),
+            pltpu.SemaphoreType.DMA((2, 2, 2)),
+            pltpu.SemaphoreType.DMA((2, n - 1)),
+            pltpu.SemaphoreType.DMA((2, n - 1)),
+        ],
+        compiler_params=pltpu.CompilerParams(
+            collective_id=1, has_side_effects=True, vmem_limit_bytes=VMEM_LIMIT
+        ),
+    )(gate_grad, up_grad, gate_w, up_w)
+
+
+def local(ring, tokens, cotangent, expert_ids, combine, w_gate, w_up, w_down, scale_vector):
     experts = lax.axis_size("expert")
     tok_count = tokens.shape[0]
     capacity = 2 * tok_count // experts + 1
@@ -45,23 +353,17 @@
         "ect,td->ecd", dispatch_half, cotangent, preferred_element_type=jnp.float32
     )
     sent_grads = (slot_weight[:, :, None] * cot_rows).astype(jnp.bfloat16)
-    got_rows, got_grads = (
-        lax.all_to_all(sent_rows, "expert", split_axis=0, concat_axis=0, tiled=True),
-        lax.all_to_all(sent_grads, "expert", split_axis=0, concat_axis=0, tiled=True),
-    )
+    sent = jnp.concatenate([sent_rows, sent_grads], axis=2)
+    got = lax.all_to_all(sent, "expert", split_axis=0, concat_axis=0, tiled=True)
     row_count = experts * capacity
+    padding = -row_count % ROW_TILE
+    x = jnp.pad(got.reshape(row_count, got.shape[2]), ((0, padding), (0, 0)))
     gate_w = w_gate[0]
     up_w = w_up[0]
     down_w = w_down[0]
-    rows_piece = lax.all_gather(got_rows, "dp", axis=2, tiled=True)
-    grads_piece = lax.all_gather(got_grads, "dp", axis=2, tiled=True)
-    piece_width = rows_piece.shape[2]
-    rows_flat = rows_piece.reshape(row_count, piece_width)
-    grads_flat = grads_piece.reshape(row_count, piece_width)
-    gate_act = jnp.dot(rows_flat, gate_w, preferred_element_type=jnp.float32)
-    up_act = jnp.dot(rows_flat, up_w, preferred_element_type=jnp.float32)
+    gate_act, up_act, grads = gather_acts(ring, x, gate_w, up_w)
     hidden_grad = lax.dot_general(
-        grads_flat, down_w, (((1,), (1,)), ((), ())), preferred_element_type=jnp.float32
+        grads, down_w, (((1,), (1,)), ((), ())), preferred_element_type=jnp.float32
     )
     sigmoid_gate = jax.nn.sigmoid(gate_act)
     silu_gate = gate_act * sigmoid_gate
@@ -71,10 +373,8 @@
     gate_grad = (
         scaled_grad * up_act * sigmoid_gate * (1.0 + gate_act * (1.0 - sigmoid_gate))
     ).astype(jnp.bfloat16)
-    partial_value = lax.dot_general(
-        gate_grad, gate_w, (((1,), (1,)), ((), ())), preferred_element_type=jnp.float32
-    ) + lax.dot_general(up_grad, up_w, (((1,), (1,)), ((), ())), preferred_element_type=jnp.float32)
-    summed = lax.psum_scatter(partial_value, "dp", scatter_dimension=1, tiled=True)
+    halves = scatter_rows(ring, gate_grad, up_grad, gate_w, up_w)
+    summed = jnp.concatenate([halves[0], halves[1]], axis=1)[:row_count]
     slot_part = summed.reshape(experts, capacity, summed.shape[1])
     returned = lax.all_to_all(slot_part, "expert", split_axis=0, concat_axis=0, tiled=True)
     token_grads = combine_slots(returned.reshape(row_count, returned.shape[2]), flat_index)
@@ -93,7 +393,7 @@
         P("expert", "dp"),
     )
     return jax.shard_map(
-        local,
+        functools.partial(local, ring_order(mesh)),
         mesh=mesh,
         in_specs=placed,
         out_specs=(P("expert", "dp"), P("expert", "dp")),

time: 429 us -> 237 us (0.55)
  waiting for transfers between devices: 285 us -> 23.3 us
  Pallas kernels: 0 us -> 171 us
  matrix products: 77.4 us -> 20.2 us
  blocking collectives: 25.6 us -> 0 us
  between operations: 14 us -> 0.82 us
  local copies, waits for them, and re-layouts: 18.1 us -> 8.24 us
    pallas_call x0 -> x2, Pallas kernels: none -> 171 us  [the longest x1 107 us: gather_acts(): pl.pallas_call(functools.partial(gather_kernel, ring, tile), out_shape=(j...]
    reduce_scatter x1 -> x0, waiting for transfers between devices: 148 us -> none  [local(): lax.psum_scatter(partial_value, 'dp', scatter_dimension=1, tiled=True)]
    all_gather x2 -> x0, waiting for transfers between devices: 123 us -> none  [the longest x1 65.7 us: local(): grads_piece = lax.all_gather(got_grads, 'dp', axis=2, tiled=True)]
    dot_general x5 -> x1, matrix products: 76.8 us -> 18.6 us  [local(): lax.dot_general(grads, down_w, (((1,), (1,)), ((), ())), preferred_elemen...]
    all_to_all x2 -> x0, blocking collectives: 25.6 us -> none  [the longest x1 13.3 us: local(): lax.all_to_all(sent_grads, 'expert', split_axis=0, concat_axis=0, tiled=T...]
    all_to_all x0 -> x1, waiting for transfers between devices: none -> 15.1 us  [local(): lax.all_to_all(sent, 'expert', split_axis=0, concat_axis=0, tiled=True)]
    reshape x3 -> x2, local copies, waits for them, and re-layouts: 10.8 us -> 0.3 us  [the longest x1 0.29 us: local(): x = jnp.pad(got.reshape(row_count, got.shape[2]), ((0, padding), (0, 0)))]
    all_to_all x1, waiting for transfers between devices: 14.2 us -> 8.19 us  [local(): lax.all_to_all(slot_part, 'expert', split_axis=0, concat_axis=0, tiled=True)]
  transfers between devices with their start and end apart: 4 -> 2, of which waited for: 4 -> 2; matrix products, arithmetic and copies ran while one was open for 5% -> 0% of each run, Pallas kernels for 0% -> 0%
where the time goes in v1:
time: 237 us
  Pallas kernels  171 us (72%)
  waiting for transfers between devices  23.3 us (10%)
  matrix products  20.2 us (9%)
  local copies, waits for them, and re-layouts  8.24 us (3%)
  starting transfers between devices  7.73 us (3%)
  other arithmetic  5.62 us (2%)
    pallas_call x1, Pallas kernels, gather_acts(): pl.pallas_call(functools.partial(gather_kernel, ring, tile), out_shape=(j...  107 us
    pallas_call x1, Pallas kernels, scatter_rows(): pl.pallas_call(functools.partial(scatter_kernel, ring), out_shape=jax.Sha...  64.2 us
    dot_general x1, matrix products, local(): lax.dot_general(grads, down_w, (((1,), (1,)), ((), ())), preferred_elemen...  18.6 us
    all_to_all x1, waiting for transfers between devices, local(): lax.all_to_all(sent, 'expert', split_axis=0, concat_axis=0, tiled=True)  15.1 us
    all_to_all x1, waiting for transfers between devices, local(): lax.all_to_all(slot_part, 'expert', split_axis=0, concat_axis=0, tiled=True)  8.19 us
  transfers between devices with their start and end apart: 2, of which 2 were waited for; matrix products, arithmetic and copies ran while one was open for 0% of the time, Pallas kernels for 0%

profile of v1, /device:TPU:0, one launch (start us, length us, event | category | flops | bytes accessed | tf_op | source)
XLA Modules:
  0.0 237.0 jit_solution(15549795996586648786)
XLA Ops:
  0.6 0.9 copy.30
  1.7 1.2 reduce-window.6
  2.9 0.2 slice_reduce_fusion
  3.1 0.7 convert_convert_fusion
  3.8 0.2 reduce-window.9
  4.4 1.3 multiply_reduce_fusion.1
  5.8 0.3 convolution_convert_fusion
  6.2 1.3 fusion.3
  7.4 1.1 pad_maximum_fusion
  8.5 4.3 %all-to-all-start = ((bf16[4,129,1024]{2,1,0:T(8,128)(2,1)}), bf16[4,129,1024]{2,1,0:T(8,128)(2,1)S(1)}, u32[]{:S(2)}, u32[]{:S(2)}) async-start(bf16[4,129,1024]{2,1,0:T(8,128)(2,1)} %pad_maximum_fusion), calls=%async_computation | async-start | bytes 2228224 | tf_op jit(solution)/shard_map/all_to_all | solution.py:357
  12.8 15.1 %all-to-all-done = bf16[4,129,1024]{2,1,0:T(8,128)(2,1)S(1)} async-done(((bf16[4,129,1024]{2,1,0:T(8,128)(2,1)}), bf16[4,129,1024]{2,1,0:T(8,128)(2,1)S(1)}, u32[]{:S(2)}, u32[]{:S(2)}) %all-to-all-start) | async-done | bytes 1056800 | tf_op jit(solution)/shard_map/all_to_all | solution.py:357
  27.9 0.3 reshape.200
  28.2 1.1 pad.4.x_ref
  29.3 106.8 %shard_map.95 = (f32[528,1792]{1,0:T(8,128)}, f32[528,1792]{1,0:T(8,128)}, bf16[528,4096]{1,0:T(8,128)(2,1)}) custom-call(bf16[528,1024]{1,0:T(8,128)(2,1)} %pad.4.x_ref, bf16[4096,1792]{1,0:T(8,128)(2,1)} %bitcast.35, bf16[4096,1792]{1,0:T(8,128)(2,1)} %bitcast.37), custom_call_target="tpu_custom_call" | custom-call | tf_op jit(solution)/shard_map/pallas_call | solution.py:202
  136.2 18.6 %multiply_reduce_fusion = (f32[1792]{0:T(1024)S(1)}, bf16[528,1792]{1,0:T(8,128)(2,1)}, bf16[528,1792]{1,0:T(8,128)(2,1)}) fusion(f32[528,1792]{1,0:T(8,128)} %get-tuple-element.6, f32[528,1792]{1,0:T(8,128)} %get-tuple-element.7, f32[1792]{0:T(1024)S(1)} %reduce.4, bf16[528,4096]{1,0:T(8,128)(2,1)} %get-tuple-element.5, bf16[1,1792,4096]{2,1,0:T(8,128)(2,1)} %param.14), kind=kOutput, calls=%fused_computation.3 | convolution fusion | flops 7767156736 | bytes 30373888 | tf_op jit(solution)/shard_map/dot_general | solution.py:365
  154.8 64.2 %shard_map.96 = bf16[2,528,256]{2,1,0:T(8,128)(2,1)} custom-call(bf16[528,1792]{1,0:T(8,128)(2,1)} %get-tuple-element.13.gate_grad, bf16[528,1792]{1,0:T(8,128)(2,1)} %get-tuple-element.14.up_grad, bf16[4096,1792]{1,0:T(8,128)(2,1)} %bitcast.36, bf16[4096,1792]{1,0:T(8,128)(2,1)} %bitcast.38), custom_call_target="tpu_custom_call" | custom-call | tf_op jit(solution)/shard_map/pallas_call | solution.py:321
  219.1 1.1 slice_bitcast_fusion.1
  220.2 0.9 reshape.201
  221.1 3.5 %all-to-all-start.1 = ((bf16[4,129,512]{2,1,0:T(8,128)(2,1)}), bf16[4,129,512]{2,1,0:T(8,128)(2,1)S(1)}, u32[]{:S(2)}, u32[]{:S(2)}) async-start(bf16[4,129,512]{2,1,0:T(8,128)(2,1)} %reshape.201), calls=%async_computation.1 | async-start | bytes 1114112 | tf_op jit(solution)/shard_map/all_to_all | solution.py:379
  224.9 0.6 broadcast_in_dim.19
  225.5 8.2 %all-to-all-done.1 = bf16[4,129,512]{2,1,0:T(8,128)(2,1)S(1)} async-done(((bf16[4,129,512]{2,1,0:T(8,128)(2,1)}), bf16[4,129,512]{2,1,0:T(8,128)(2,1)S(1)}, u32[]{:S(2)}, u32[]{:S(2)}) %all-to-all-start.1) | async-done | bytes 528416 | tf_op jit(solution)/shard_map/all_to_all | solution.py:379
  233.9 2.0 gather_fusion
  235.9 0.2 gather.7
  236.2 0.8 fusion.6
  (29 shorter events, 1.3 us)
Async XLA Ops:
  0.6 5.2 %copy-start = (bf16[256,512]{1,0:T(8,128)(2,1)S(1)}, bf16[256,512]{1,0:T(8,128)(2,1)}, u32[]{:S(2)}) copy-start(bf16[256,512]{1,0:T(8,128)(2,1)} %param.8) | copy-start | bytes 786436
  4.4 8.5 %copy-start.3 = (f32[1,1792]{1,0:T(1,128)S(1)}, f32[1,1792]{1,0:T(1,128)}, u32[]{:S(2)}) copy-start(f32[1,1792]{1,0:T(1,128)} %param.15) | copy-start | bytes 21508
  8.5 19.4 %all-to-all-start = ((bf16[4,129,1024]{2,1,0:T(8,128)(2,1)}), bf16[4,129,1024]{2,1,0:T(8,128)(2,1)S(1)}, u32[]{:S(2)}, u32[]{:S(2)}) async-start(bf16[4,129,1024]{2,1,0:T(8,128)(2,1)} %pad_maximum_fusion), calls=%async_computation | async-start | bytes 2228224 | tf_op jit(solution)/shard_map/all_to_all | solution.py:357
  219.0 5.6 %copy-start.2 = (s32[256,2]{0,1:T(2,128)S(1)}, s32[256,2]{0,1:T(2,128)}, u32[]{:S(2)}) copy-start(s32[256,2]{0,1:T(2,128)} %param.10) | copy-start | bytes 6148
  221.1 12.6 %all-to-all-start.1 = ((bf16[4,129,512]{2,1,0:T(8,128)(2,1)}), bf16[4,129,512]{2,1,0:T(8,128)(2,1)S(1)}, u32[]{:S(2)}, u32[]{:S(2)}) async-start(bf16[4,129,512]{2,1,0:T(8,128)(2,1)} %reshape.201), calls=%async_computation.1 | async-start | bytes 1114112 | tf_op jit(solution)/shard_map/all_to_all | solution.py:379
  233.7 3.3 %copy-start.1 = (bf16[256,512]{1,0:T(8,128)(2,1)S(1)}, bf16[256,512]{1,0:T(8,128)(2,1)}, u32[]{:S(2)}) copy-start(bf16[256,512]{1,0:T(8,128)(2,1)} %param.8) | copy-start | bytes 786436
